TPU v7x, 256 devices: a whole 4x4x8 slice. The times are simulated.
256 devices in a mesh: section: 2 (over core), seq: 16 (over x, y), head: 8 (over z).
Axes of the slice: x: 4, y: 4, z: 8, core: 2. Of those that a mesh axis runs over, the one named last changes fastest.
Arguments:
- x_in: bfloat16 [2, 4096, 8192], P('section', 'seq', 'head'), may hold values from -6 to 6
- b_in: bfloat16 [2, 4096, 2048], P('section', 'seq', 'head'), may hold values from -6 to 6
- c_in: bfloat16 [2, 4096, 2048], P('section', 'seq', 'head'), may hold values from -6 to 6
- z_in: bfloat16 [2, 4096, 8192], P('section', 'seq', 'head'), may hold values from -6 to 6
- dt_raw: float32 [2, 128, 4096], P('section', 'head', 'seq'), may hold values from -5 to 5
- conv_x: float32 [2, 4, 8192], P('section', None, 'head'), may hold values from -3 to 3
- conv_b: float32 [2, 4, 2048], P('section', None, 'head'), may hold values from -3 to 3
- conv_c: float32 [2, 4, 2048], P('section', None, 'head'), may hold values from -3 to 3
- a_rate: float32 [2, 128], P('section', 'head'), may hold values from 0.0001 to 1
- dt_bias: float32 [2, 128], P('section', 'head'), may hold values from -3 to -0.5
- skip_d: float32 [2, 128], P('section', 'head'), may hold values from 0.5 to 2
- norm_gain: float32 [2, 8192], P('section', 'head'), may hold values from 0.25 to 1.75
- out_weight: bfloat16 [2, 8192, 8192], P('section', 'head', 'seq'), may hold values from -0.0625 to 0.0625
Outputs:
- mixed: bfloat16 [2, 4096, 8192], P('section', ('seq', 'head'))
All inputs are finite; a program needn't handle non-finite values.
Results may differ from a plain program's by a relative error of at most 0.007.
Values may be sent and summed in bfloat16 or wider, within the bound.
A program may use at most 128 MiB of HBM per device.

v0:
```python
import jax
import jax.numpy as jnp
from jax import lax
from jax.sharding import Mesh
from jax.sharding import PartitionSpec as P

N = 256
SEQ = ("seq_0", "seq_1")
SEQ_HEAD = ("seq_0", "seq_1", "head")
epsilon = 1e-05


def passed_along(block, axis, distance):
    devices = range(lax.axis_size(axis))
    route = [(i - distance, i) for i in devices if i - distance in devices]
    return lax.ppermute(block, axis, route)


def neutral_like(x, identity):
    return jax.tree.map(
        lambda part, zero: jnp.zeros_like(part) + jnp.asarray(zero, part.dtype), x, identity
    )


def entering(x, axes, combine, identity):
    before = start = neutral_like(x, identity)
    so_far = x
    for axis in reversed(axes):
        size, place = (lax.axis_size(axis), lax.axis_index(axis))
        pieces = jax.tree.map(lambda part: lax.all_gather(part, axis), so_far)
        inside, so_far = (start, start)
        for k in range(size):
            passed = k < place
            so_far = combine(so_far, jax.tree.map(lambda part: part[k], pieces))
            inside = jax.tree.map(lambda new, old: jnp.where(passed, new, old), so_far, inside)
        before = combine(inside, before)
    return before


def from_everyone(x, axis):
    size = lax.axis_size(axis)
    return lax.all_to_all(jnp.broadcast_to(x[None], (size, *x.shape)), axis, 0, 0, tiled=True)


def in_order(pieces, dim):
    pieces = jnp.moveaxis(pieces, 0, dim)
    shape = pieces.shape
    return pieces.reshape(*shape[:dim], shape[dim] * shape[dim + 1], *shape[dim + 2 :])


def collect(x, axis, dim):
    pieces = from_everyone(x, axis)
    return in_order(pieces, dim)


def passed_along_2(block, axis, distance):
    devices = range(lax.axis_size(axis))
    route = [((i - distance) % len(devices), i) for i in devices]
    return lax.ppermute(block, axis, route)


def conv_silu(padded, kernel, length):
    kernel_taps = kernel.shape[0]
    summed = jnp.zeros((length, padded.shape[1]), jnp.float32)
    for offset in range(kernel_taps):
        summed = summed + kernel[offset] * padded[offset : offset + length].astype(jnp.float32)
    return jax.nn.silu(summed).astype(jnp.bfloat16)


def carry_combine(earlier, latter):
    return (earlier[0] * latter[0], latter[0][:, :, None, None] * earlier[1] + latter[1])


def per_device(
    x_in,
    b_in,
    c_in,
    z_in,
    dt_raw,
    conv_x,
    conv_b,
    conv_c,
    a_rate,
    dt_bias,
    skip_d,
    norm_gain,
    out_weight,
):
    x_local = x_in[0]
    b_local = b_in[0]
    c_local = c_in[0]
    length = x_local.shape[0]
    kernel_taps = conv_x.shape[1]
    x_cols = x_local.shape[1]
    b_cols = b_local.shape[1]
    edge_rows = jnp.concatenate(
        [
            x_local[length - kernel_taps + 1 :],
            b_local[length - kernel_taps + 1 :],
            c_local[length - kernel_taps + 1 :],
        ],
        axis=1,
    )
    before = passed_along(edge_rows, SEQ, 1)
    x_conv = conv_silu(jnp.concatenate([before[:, :x_cols], x_local], axis=0), conv_x[0], length)
    b_conv = conv_silu(
        jnp.concatenate([before[:, x_cols : x_cols + b_cols], b_local], axis=0), conv_b[0], length
    )
    c_conv = conv_silu(
        jnp.concatenate([before[:, x_cols + b_cols :], c_local], axis=0), conv_c[0], length
    )
    head_count = dt_raw.shape[1]
    group_count = b_cols // N
    per_group = head_count // group_count
    head_dim = x_cols // head_count
    step_size = jax.nn.softplus(dt_raw[0] + dt_bias[0][:, None])
    log_decay = jnp.cumsum(-a_rate[0][:, None] * step_size, axis=1)
    x_groups = x_conv.reshape(length, group_count, per_group, head_dim)
    b_groups = b_conv.reshape(length, group_count, N)
    c_groups = c_conv.reshape(length, group_count, N)
    log_groups = log_decay.reshape(group_count, per_group, length)
    step_groups = step_size.reshape(group_count, per_group, length)
    scores = jnp.einsum("tgn,ugn->gtu", c_groups, b_groups, preferred_element_type=jnp.float32)
    causal = jnp.arange(length)[:, None] >= jnp.arange(length)[None, :]
    spread_log = log_groups[:, :, :, None] - log_groups[:, :, None, :]
    damping = jnp.where(causal, jnp.exp(jnp.minimum(spread_log, 0.0)), 0.0)
    weights = (damping * step_groups[:, :, None, :] * scores[:, None]).astype(jnp.bfloat16)
    inside = jnp.einsum("gjtu,ugjp->tgjp", weights, x_groups, preferred_element_type=jnp.float32)
    to_end = jnp.exp(log_groups[:, :, -1:] - log_groups) * step_groups
    x_weighted = (
        x_groups.astype(jnp.float32) * jnp.transpose(to_end, (2, 0, 1))[..., None]
    ).astype(jnp.bfloat16)
    block_sum = jnp.einsum(
        "ugjp,ugn->gjpn", x_weighted, b_groups, preferred_element_type=jnp.float32
    )
    block_decay = jnp.exp(log_groups[:, :, -1])
    identity = (jnp.ones_like(block_decay), jnp.zeros_like(block_sum))
    carried_decay, carried = entering((block_decay, block_sum), SEQ, carry_combine, identity)
    carried_b = carried.astype(jnp.bfloat16)
    outside = jnp.einsum("tgn,gjpn->tgjp", c_groups, carried_b, preferred_element_type=jnp.float32)
    outside = outside * jnp.transpose(jnp.exp(log_groups), (2, 0, 1))[..., None]
    skip_term = skip_d[0].reshape(group_count, per_group)
    out_ssm = inside + outside + skip_term[None, :, :, None] * x_groups.astype(jnp.float32)
    gate_act = jax.nn.silu(z_in[0].astype(jnp.float32)).reshape(
        length, group_count, per_group * head_dim
    )
    gated = out_ssm.reshape(length, group_count, per_group * head_dim) * gate_act
    inverse_rms = lax.rsqrt(jnp.mean(gated * gated, axis=2, keepdims=True) + epsilon)
    hidden = ((gated * inverse_rms).reshape(length, x_cols) * norm_gain[0]).astype(jnp.bfloat16)
    local_weight = out_weight[0]
    full_columns = lax.all_gather(local_weight, "head", axis=0, tiled=True)
    owned_rows = lax.all_to_all(hidden, "head", split_axis=0, concat_axis=1, tiled=True)
    column_block = jnp.dot(
        collect(owned_rows, SEQ, 0), full_columns, preferred_element_type=jnp.float32
    ).astype(jnp.bfloat16)
    mixed = lax.all_to_all(column_block, SEQ, split_axis=0, concat_axis=1, tiled=True)
    passed = passed_along_2(mixed, "section", 1)
    return passed[None]


def solution(mesh):
    finer = Mesh(
        mesh.devices.reshape(mesh.shape["section"], 4, 4, mesh.shape["head"]),
        ("section", "seq_0", "seq_1", "head"),
    )
    return jax.shard_map(
        per_device,
        mesh=finer,
        in_specs=(
            P("section", SEQ, "head"),
            P("section", SEQ, "head"),
            P("section", SEQ, "head"),
            P("section", SEQ, "head"),
            P("section", "head", SEQ),
            P("section", None, "head"),
            P("section", None, "head"),
            P("section", None, "head"),
            P("section", "head"),
            P("section", "head"),
            P("section", "head"),
            P("section", "head"),
            P("section", "head", SEQ),
        ),
        out_specs=P("section", SEQ_HEAD, None),
        check_vma=False,
    )
```

profile of v0, /device:TPU:1, one launch (start us, length us, event | category | flops | bytes accessed | tf_op | source)
XLA Modules:
  0.0 360.7 jit_solution(4623957862641445590)
XLA Ops:
  8.2 4.0 %collective-permute-start = (bf16[3,1536]{0,1:T(8,128)(2,1)S(1)}, bf16[3,1536]{0,1:T(8,128)(2,1)S(1)}, u32[]{:S(2)}, u32[]{:S(2)}) collective-permute-start(bf16[3,1536]{0,1:T(8,128)(2,1)S(1)} %copy.48), channel_id=1, source_target_pairs={{0,8},{8,16},{16,24},{24,32},{32,40},{40,48},{48,56},{56,64},{64,7... | collective-permute-start | bytes 27656 | tf_op jit(solution)/shard_map/ppermute | solution.py:16
  18.0 1.2 copy.49
  20.2 1.4 multiply_convert_fusion.6
  21.5 1.5 fusion.24
  23.0 1.3 fusion.50
  24.4 9.0 %all-gather = f32[4,16,1]{1,2,0:T(1,128)S(1)} all-gather(f32[1,16,1]{1,2,0:T(1,128)S(1)} %exp.90), channel_id=2, replica_groups=mesh['section'=2,'seq_0'=4,'seq_1'=4,'head'=8] {'seq_1'}, dimensions={0}, use_global_device_ids=true | all-gather | bytes 320 | tf_op jit(solution)/shard_map/all_gather | solution.py:30
  33.4 46.4 %all-gather.9.cloned.1.call-done = f32[64,64,256]{2,1,0:T(8,128)} async-done(((f32[16,64,256]{2,1,0:T(8,128)}), f32[64,64,256]{2,1,0:T(8,128)}) %all-gather.9.cloned.1.call-update) | async-done | bytes 4194320 | tf_op jit(solution)/shard_map/all_gather | solution.py:30
  79.8 3.6 %fusion.20 = f32[1,1,16,64,256]{4,3,2,1,0:T(8,128)} fusion(f32[64,64,256]{2,1,0:T(8,128)} %all-gather.9.cloned.1.call-done, f32[16]{0:T(128)S(1)} %get-tuple-element.31, f32[16]{0:T(128)S(1)} %get-tuple-element.30, f32[16]{0:T(128)S(1)} %get-tuple-element.24, f32[16]{0:T(128)S(1)} %get-tuple-element.32), kind=kLoop, calls=%fused_computation.25 | loop fusion | flops 1835008 | bytes 5243136 | tf_op jit(solution)/shard_map/add | solution.py:71
  84.5 1.1 convert_element_type.148
  85.6 7.6 %all_gather.22 = f32[4,1,16]{2,1,0:T(1,128)S(1)} all-gather(f32[1,1,16]{2,1,0:T(1,128)S(1)} %get-tuple-element.29), channel_id=1, replica_groups=mesh['section'=2,'seq_0'=4,'seq_1'=4,'head'=8] {'seq_0'}, dimensions={0}, use_global_device_ids=true | all-gather | bytes 320 | tf_op jit(solution)/shard_map/all_gather | solution.py:30
  94.0 2.5 fusion.9
  96.5 38.2 %all-gather.7.cloned.1.call-done = f32[4,1,16,64,256]{4,3,2,1,0:T(8,128)} async-done(((f32[1,1,16,64,256]{4,3,2,1,0:T(8,128)}), f32[4,1,16,64,256]{4,3,2,1,0:T(8,128)}) %all-gather.7.cloned.1.call-update) | async-done | bytes 4194320 | tf_op jit(solution)/shard_map/all_gather | solution.py:30
  134.7 5.7 %multiply_reduce_fusion = (f32[256]{0:T(256)S(1)}, f32[256,1,16,64]{0,3,2,1:T(8,128)}) fusion(f32[256,1,16,64]{0,3,2,1:T(8,128)S(1)} %bitcast.184, f32[16]{0:T(128)S(1)} %bitcast.209, f32[256,1,16,64]{0,3,2,1:T(8,128)} %fusion.9, f32[256,16]{0,1:T(8,128)S(1)} %get-tuple-element.9, bf16[256,256]{1,0:T(8,128)(2,1)S(1)} %multiply_convert_fusion.7, ...), kind=kOutput, calls=%fused_computation.35 | convolution fusion | flops 143392512 | bytes 12207688 | tf_op jit(solution)/shard_map/tgn,gjpn->tgjp/dot_general | solution.py:140
  140.4 2.5 copy.56
  143.6 1.6 multiply_convert_fusion.4
  145.2 29.7 %all_to_all.37 = bf16[8,32,1024]{2,1,0:T(8,128)(2,1)S(1)} all-to-all(bf16[8,32,1024]{2,1,0:T(8,128)(2,1)S(1)} %multiply_convert_fusion.4), channel_id=1, replica_groups=mesh['section'=2,'seq_0'=4,'seq_1'=4,'head'=8] {'head'}, dimensions={0} | all-to-all | bytes 1048576 | tf_op jit(solution)/shard_map/all_to_all | solution.py:152
  174.9 4.2 %broadcast_in_dim.36 = bf16[16,32,8192]{2,1,0:T(8,128)(2,1)} broadcast(bf16[32,8192]{1,0:T(8,128)(2,1)S(1)} %bitcast.181), dimensions={1,2} | broadcast | bytes 8912896 | tf_op jit(solution)/shard_map/broadcast_in_dim | solution.py:42
  179.2 5.7 %all-to-all-start.1 = ((bf16[16,32,8192]{2,1,0:T(8,128)(2,1)}), bf16[16,32,8192]{2,1,0:T(8,128)(2,1)}, u32[]{:S(2)}, u32[]{:S(2)}) async-start(bf16[16,32,8192]{2,1,0:T(8,128)(2,1)} %broadcast_in_dim.36), calls=%async_computation.1 | async-start | bytes 16777216 | tf_op jit(solution)/shard_map/all_to_all | solution.py:42
  184.8 57.4 %all-gather.11.cloned.1.call-done = bf16[1,8192,512]{2,1,0:T(8,128)(2,1)} async-done(((bf16[1,1024,512]{2,1,0:T(8,128)(2,1)}), bf16[1,8192,512]{2,1,0:T(8,128)(2,1)}) %all-gather.11.cloned.1.call-update) | async-done | bytes 8388624 | tf_op jit(solution)/shard_map/all_gather | solution.py:151
  242.2 74.1 %all-to-all-done.1 = bf16[16,32,8192]{2,1,0:T(8,128)(2,1)} async-done(((bf16[16,32,8192]{2,1,0:T(8,128)(2,1)}), bf16[16,32,8192]{2,1,0:T(8,128)(2,1)}, u32[]{:S(2)}, u32[]{:S(2)}) %all-to-all-start.1) | async-done | bytes 8388640 | tf_op jit(solution)/shard_map/all_to_all | solution.py:42
  316.4 10.2 %fusion.13 = bf16[512,512]{1,0:T(8,128)(2,1)S(1)} fusion(bf16[512,8192]{1,0:T(8,128)(2,1)} %bitcast.55, bf16[1,8192,512]{2,1,0:T(8,128)(2,1)} %all-gather.11.cloned.1.call-done), kind=kOutput, calls=%fused_computation.15 | convolution fusion | flops 4295229440 | bytes 17301504 | tf_op jit(solution)/shard_map/dot_general | solution.py:153
  326.6 19.9 %all_to_all.38 = bf16[16,32,512]{2,1,0:T(8,128)(2,1)S(1)} all-to-all(bf16[16,32,512]{2,1,0:T(8,128)(2,1)S(1)} %bitcast.189), channel_id=1, replica_groups=mesh['section'=2,'seq_0'=4,'seq_1'=4,'head'=8] {'seq_0','seq_1'}, dimensions={0} | all-to-all | bytes 1048576 | tf_op jit(solution)/shard_map/all_to_all | solution.py:156
  346.6 5.2 %collective-permute-start.1 = (bf16[32,8192]{1,0:T(8,128)(2,1)S(1)}, bf16[32,8192]{1,0:T(8,128)(2,1)S(1)}, u32[]{:S(2)}, u32[]{:S(2)}) collective-permute-start(bf16[32,8192]{1,0:T(8,128)(2,1)S(1)} %bitcast.187), channel_id=1, source_target_pairs={{128,0},{0,128},{129,1},{1,129},{130,2},{2,130},{131,3},{3,131},{1... | collective-permute-start | bytes 1572872 | tf_op jit(solution)/shard_map/ppermute | solution.py:59
  351.8 1.5 collective-permute-done.1
  (63 shorter events, 11.6 us)
Async XLA Ops:
  6.5 73.3 %all-gather.9.cloned.1.call-start = ((), (), s32[]{:S(2)}) async-start(), calls=%async_computation.4 | async-start | bytes 5242880 | tf_op jit(solution)/shard_map/all_gather | solution.py:30
  8.2 11.8 %collective-permute-start = (bf16[3,1536]{0,1:T(8,128)(2,1)S(1)}, bf16[3,1536]{0,1:T(8,128)(2,1)S(1)}, u32[]{:S(2)}, u32[]{:S(2)}) collective-permute-start(bf16[3,1536]{0,1:T(8,128)(2,1)S(1)} %copy.48), channel_id=1, source_target_pairs={{0,8},{8,16},{16,24},{24,32},{32,40},{40,48},{48,56},{56,64},{64,7... | collective-permute-start | bytes 27656 | tf_op jit(solution)/shard_map/ppermute | solution.py:16
  24.3 59.9 %copy-start.1 = (bf16[1,256,1024]{2,1,0:T(8,128)(2,1)S(1)}, bf16[1,256,1024]{2,1,0:T(8,128)(2,1)}, u32[]{:S(2)}) copy-start(bf16[1,256,1024]{2,1,0:T(8,128)(2,1)} %param.16) | copy-start | bytes 1572868
  24.3 110.4 %all-gather.7.cloned.1.call-start = ((), (), s32[]{:S(2)}) async-start(), calls=%async_computation.3 | async-start | bytes 5242880 | tf_op jit(solution)/shard_map/all_gather | solution.py:30
  79.8 13.4 %copy-start.6 = (f32[1,4,256]{2,1,0:T(4,128)S(1)}, f32[1,4,256]{2,1,0:T(4,128)}, u32[]{:S(2)}) copy-start(f32[1,4,256]{2,1,0:T(4,128)} %param.20) | copy-start | bytes 12292
  79.8 13.4 %copy-start.2 = (f32[1,16,256]{2,1,0:T(8,128)S(1)}, f32[1,16,256]{2,1,0:T(8,128)}, u32[]{:S(2)}) copy-start(f32[1,16,256]{2,1,0:T(8,128)} %param.17) | copy-start | bytes 49156
  79.8 13.4 %copy-start.4 = (f32[1,16]{1,0:T(1,128)S(1)}, f32[1,16]{1,0:T(1,128)}, u32[]{:S(2)}) copy-start(f32[1,16]{1,0:T(1,128)} %param.22) | copy-start | bytes 196
  79.8 13.7 %copy-start.3 = (bf16[1,256,256]{2,1,0:T(8,128)(2,1)S(1)}, bf16[1,256,256]{2,1,0:T(8,128)(2,1)}, u32[]{:S(2)}) copy-start(bf16[1,256,256]{2,1,0:T(8,128)(2,1)} %param.15) | copy-start | bytes 393220
  83.5 158.7 %all-gather.11.cloned.1.call-start = ((), (), s32[]{:S(2)}) async-start(), calls=%async_computation.5 | async-start | bytes 9437184 | tf_op jit(solution)/shard_map/all_gather | solution.py:151
  93.7 41.0 %copy-start = (f32[1,1,16,64,256]{4,3,2,1,0:T(8,128)S(1)}, f32[1,1,16,64,256]{4,3,2,1,0:T(8,128)}, u32[]{:S(2)}) copy-start(f32[1,1,16,64,256]{4,3,2,1,0:T(8,128)} %fusion.20) | copy-start | bytes 3145732
  93.7 41.0 %copy-start.7 = (f32[1,16]{1,0:T(1,128)S(1)}, f32[1,16]{1,0:T(1,128)}, u32[]{:S(2)}) copy-start(f32[1,16]{1,0:T(1,128)} %param.23) | copy-start | bytes 196
  140.4 3.2 copy-start.5
  179.2 137.2 %all-to-all-start.1 = ((bf16[16,32,8192]{2,1,0:T(8,128)(2,1)}), bf16[16,32,8192]{2,1,0:T(8,128)(2,1)}, u32[]{:S(2)}, u32[]{:S(2)}) async-start(bf16[16,32,8192]{2,1,0:T(8,128)(2,1)} %broadcast_in_dim.36), calls=%async_computation.1 | async-start | bytes 16777216 | tf_op jit(solution)/shard_map/all_to_all | solution.py:42
  346.6 6.7 %collective-permute-start.1 = (bf16[32,8192]{1,0:T(8,128)(2,1)S(1)}, bf16[32,8192]{1,0:T(8,128)(2,1)S(1)}, u32[]{:S(2)}, u32[]{:S(2)}) collective-permute-start(bf16[32,8192]{1,0:T(8,128)(2,1)S(1)} %bitcast.187), channel_id=1, source_target_pairs={{128,0},{0,128},{129,1},{1,129},{130,2},{2,130},{131,3},{3,131},{1... | collective-permute-start | bytes 1572872 | tf_op jit(solution)/shard_map/ppermute | solution.py:59
Sparse Core Ops, SparseCore 0:
  24.5 55.3 all-gather.8
  83.6 51.0 all-gather.6
  136.5 105.6 all-gather.10
where the time goes:
time: 361 us
  waiting for transfers between devices  219 us (61%)
  blocking collectives  66.2 us (18%)
  matrix products  19.9 us (6%)
  starting transfers between devices  15 us (4%)
  local copies, waits for them, and re-layouts  14.5 us (4%)
  between operations  13.4 us (4%)
  other arithmetic  12.5 us (3%)
    all_gather x2, waiting for transfers between devices, entering(): pieces = jax.tree.map(lambda part: lax.all_gather(part, axis), so_far)  84.7 us
    all_to_all x1, waiting for transfers between devices, from_everyone(): lax.all_to_all(jnp.broadcast_to(x[None], (size, *x.shape)), axis, 0, 0, t...  74.1 us
    all_gather x1, waiting for transfers between devices, per_device(): full_columns = lax.all_gather(local_weight, 'head', axis=0, tiled=True)  57.4 us
    all_to_all x1, blocking collectives, per_device(): lax.all_to_all(hidden, 'head', split_axis=0, concat_axis=1, tiled=True)  29.7 us
    all_to_all x1, blocking collectives, per_device(): lax.all_to_all(column_block, SEQ, split_axis=0, concat_axis=1, tiled=True)  19.9 us
    all_gather x2, blocking collectives, entering(): pieces = jax.tree.map(lambda part: lax.all_gather(part, axis), so_far)  16.6 us
    dot_general x1, matrix products, per_device(): jnp.dot(collect(owned_rows, SEQ, 0), full_columns, preferred_element_type...  10.2 us
  transfers between devices with their start and end apart: 6, of which 6 were waited for; matrix products, arithmetic and copies ran while one was open for 7% of the time, Pallas kernels for 0%

commit v1 on v0

--- a/solution.py
+++ b/solution.py
@@ -148,7 +148,12 @@
     inverse_rms = lax.rsqrt(jnp.mean(gated * gated, axis=2, keepdims=True) + epsilon)
     hidden = ((gated * inverse_rms).reshape(length, x_cols) * norm_gain[0]).astype(jnp.bfloat16)
     local_weight = out_weight[0]
-    full_columns = lax.all_gather(local_weight, "head", axis=0, tiled=True)
+    full_columns = jnp.concatenate(
+        lax.all_to_all(
+            jnp.stack([local_weight for _ in range(lax.axis_size("head"))], axis=0), "head", 0, 0
+        ),
+        axis=0,
+    )
     owned_rows = lax.all_to_all(hidden, "head", split_axis=0, concat_axis=1, tiled=True)
     column_block = jnp.dot(
         collect(owned_rows, SEQ, 0), full_columns, preferred_element_type=jnp.float32

time: 361 us -> 499 us (1.38)
  blocking collectives: 66.2 us -> 153 us
  waiting for transfers between devices: 219 us -> 275 us
    all_to_all x1, waiting for transfers between devices: 74.1 us -> 187 us  [per_device(): lax.all_to_all(jnp.stack([local_weight for _ in range(lax.axis_size('head...]
    all_to_all x0 -> x1, blocking collectives: none -> 100 us  [from_everyone(): lax.all_to_all(jnp.broadcast_to(x[None], (size, *x.shape)), axis, 0, 0, t...]
    all_gather x1 -> x0, waiting for transfers between devices: 57.4 us -> none  [per_device(): full_columns = lax.all_gather(local_weight, 'head', axis=0, tiled=True)]
    all_to_all x1, blocking collectives: 29.7 us -> 22.4 us  [per_device(): lax.all_to_all(hidden, 'head', split_axis=0, concat_axis=1, tiled=True)]
    all_to_all x1, blocking collectives: 19.9 us -> 13.7 us  [per_device(): lax.all_to_all(column_block, SEQ, split_axis=0, concat_axis=1, tiled=True)]
  transfers between devices with their start and end apart: 6 -> 5, of which waited for: 6 -> 5; matrix products, arithmetic and copies ran while one was open for 7% -> 2% of each run, Pallas kernels for 0% -> 0%
where the time goes in v1:
time: 499 us; the launch traced here: 498 us
  waiting for transfers between devices  275 us (55%)
  blocking collectives  153 us (31%)
  matrix products  16.6 us (3%)
  local copies, waits for them, and re-layouts  15.2 us (3%)
  between operations  13.7 us (3%)
  other arithmetic  12.7 us (3%)
  starting transfers between devices  12.3 us (2%)
    all_to_all x1, waiting for transfers between devices, per_device(): lax.all_to_all(jnp.stack([local_weight for _ in range(lax.axis_size('head...  187 us
    all_to_all x1, blocking collectives, from_everyone(): lax.all_to_all(jnp.broadcast_to(x[None], (size, *x.shape)), axis, 0, 0, t...  100 us
    all_gather x2, waiting for transfers between devices, entering(): pieces = jax.tree.map(lambda part: lax.all_gather(part, axis), so_far)  85.4 us
    all_to_all x1, blocking collectives, per_device(): lax.all_to_all(hidden, 'head', split_axis=0, concat_axis=1, tiled=True)  22.4 us
    all_gather x2, blocking collectives, entering(): pieces = jax.tree.map(lambda part: lax.all_gather(part, axis), so_far)  16.5 us
    all_to_all x1, blocking collectives, per_device(): lax.all_to_all(column_block, SEQ, split_axis=0, concat_axis=1, tiled=True)  13.7 us
  transfers between devices with their start and end apart: 5, of which 5 were waited for; matrix products, arithmetic and copies ran while one was open for 2% of the time, Pallas kernels for 0%

profile of v1, /device:TPU:1, one launch (start us, length us, event | category | flops | bytes accessed | tf_op | source)
XLA Modules:
  0.0 498.0 jit_solution(9144693629647523797)
XLA Ops:
  8.2 4.0 collective-permute-start
  18.1 1.2 copy.49
  20.2 1.4 multiply_convert_fusion.6
  21.6 1.5 fusion.19
  23.1 1.3 fusion.45
  24.5 8.9 %all-gather = f32[4,16,1]{1,2,0:T(1,128)S(1)} all-gather(f32[1,16,1]{1,2,0:T(1,128)S(1)} %exp.90), channel_id=2, replica_groups=mesh['section'=2,'seq_0'=4,'seq_1'=4,'head'=8] {'seq_1'}, dimensions={0}, use_global_device_ids=true | all-gather | bytes 320 | tf_op jit(solution)/shard_map/all_gather | solution.py:30
  33.3 46.5 %all-gather.7.cloned.1.call-done = f32[64,64,256]{2,1,0:T(8,128)} async-done(((f32[16,64,256]{2,1,0:T(8,128)}), f32[64,64,256]{2,1,0:T(8,128)}) %all-gather.7.cloned.1.call-update) | async-done | bytes 4194320 | tf_op jit(solution)/shard_map/all_gather | solution.py:30
  79.9 3.6 fusion.15
  83.8 1.2 convert_element_type.148
  84.9 7.6 %all_gather.19 = f32[4,1,16]{2,1,0:T(1,128)S(1)} all-gather(f32[1,1,16]{2,1,0:T(1,128)S(1)} %get-tuple-element.29), channel_id=1, replica_groups=mesh['section'=2,'seq_0'=4,'seq_1'=4,'head'=8] {'seq_0'}, dimensions={0}, use_global_device_ids=true | all-gather | bytes 320 | tf_op jit(solution)/shard_map/all_gather | solution.py:30
  93.3 2.5 fusion.7
  95.9 38.9 %all-gather.5.cloned.1.call-done = f32[4,1,16,64,256]{4,3,2,1,0:T(8,128)} async-done(((f32[1,1,16,64,256]{4,3,2,1,0:T(8,128)}), f32[4,1,16,64,256]{4,3,2,1,0:T(8,128)}) %all-gather.5.cloned.1.call-update) | async-done | bytes 4194320 | tf_op jit(solution)/shard_map/all_gather | solution.py:30
  134.8 5.7 %multiply_reduce_fusion = (f32[256]{0:T(256)S(1)}, f32[256,1,16,64]{0,3,2,1:T(8,128)}) fusion(f32[256,1,16,64]{0,3,2,1:T(8,128)S(1)} %bitcast.184, f32[16]{0:T(128)S(1)} %bitcast.209, f32[256,1,16,64]{0,3,2,1:T(8,128)} %fusion.7, f32[256,16]{0,1:T(8,128)S(1)} %get-tuple-element.9, bf16[256,256]{1,0:T(8,128)(2,1)S(1)} %multiply_convert_fusion.7, ...), kind=kOutput, calls=%fused_computation.33 | convolution fusion | flops 143392512 | bytes 12207688 | tf_op jit(solution)/shard_map/tgn,gjpn->tgjp/dot_general | solution.py:140
  140.5 2.5 copy.56
  143.6 1.7 multiply_convert_fusion.4
  145.3 22.4 %all_to_all.42 = bf16[8,32,1024]{2,1,0:T(8,128)(2,1)S(1)} all-to-all(bf16[8,32,1024]{2,1,0:T(8,128)(2,1)S(1)} %multiply_convert_fusion.4), channel_id=1, replica_groups=mesh['section'=2,'seq_0'=4,'seq_1'=4,'head'=8] {'head'}, dimensions={0} | all-to-all | bytes 1048576 | tf_op jit(solution)/shard_map/all_to_all | solution.py:157
  167.7 4.0 stack.3
  171.7 5.0 all-to-all-start.2
  176.7 186.8 %all-to-all-done.2 = bf16[8,1024,512]{2,1,0:T(8,128)(2,1)} async-done(((bf16[8,1024,512]{2,1,0:T(8,128)(2,1)}), bf16[8,1024,512]{2,1,0:T(8,128)(2,1)}, u32[]{:S(2)}, u32[]{:S(2)}) %all-to-all-start.2) | async-done | bytes 8388640 | tf_op jit(solution)/shard_map/all_to_all | solution.py:152
  364.5 100.4 %all_to_all.43 = bf16[16,32,8192]{2,1,0:T(8,128)(2,1)S(1)} all-to-all(bf16[16,32,8192]{2,1,0:T(8,128)(2,1)S(1)} %broadcast_in_dim.36), channel_id=1, replica_groups=mesh['section'=2,'seq_0'=4,'seq_1'=4,'head'=8] {'seq_0','seq_1'}, dimensions={0} | all-to-all | bytes 16777216 | tf_op jit(solution)/shard_map/all_to_all | solution.py:42
  464.9 6.9 %convolution_convert_fusion = bf16[512,512]{1,0:T(8,128)(2,1)S(1)} fusion(bf16[512,8192]{1,0:T(8,128)(2,1)S(1)} %bitcast.176, bf16[8192,512]{1,0:T(8,128)(2,1)} %bitcast.57), kind=kOutput, calls=%fused_computation.13 | convolution fusion | flops 4295229440 | bytes 17301504 | tf_op jit(solution)/shard_map/dot_general | solution.py:158
  471.8 13.7 %all_to_all.44 = bf16[16,32,512]{2,1,0:T(8,128)(2,1)S(1)} all-to-all(bf16[16,32,512]{2,1,0:T(8,128)(2,1)S(1)} %bitcast.189), channel_id=1, replica_groups=mesh['section'=2,'seq_0'=4,'seq_1'=4,'head'=8] {'seq_0','seq_1'}, dimensions={0} | all-to-all | bytes 1048576 | tf_op jit(solution)/shard_map/all_to_all | solution.py:161
  485.5 3.3 collective-permute-start.1
  488.8 1.5 collective-permute-done.1
  (64 shorter events, 11.8 us)
Async XLA Ops:
  6.5 73.3 %all-gather.7.cloned.1.call-start = ((), (), s32[]{:S(2)}) async-start(), calls=%async_computation.5 | async-start | bytes 5242880 | tf_op jit(solution)/shard_map/all_gather | solution.py:30
  8.2 11.8 %collective-permute-start = (bf16[3,1536]{0,1:T(8,128)(2,1)S(1)}, bf16[3,1536]{0,1:T(8,128)(2,1)S(1)}, u32[]{:S(2)}, u32[]{:S(2)}) collective-permute-start(bf16[3,1536]{0,1:T(8,128)(2,1)S(1)} %copy.48), channel_id=1, source_target_pairs={{0,8},{8,16},{16,24},{24,32},{32,40},{40,48},{48,56},{56,64},{64,7... | collective-permute-start | bytes 27656 | tf_op jit(solution)/shard_map/ppermute | solution.py:16
  23.1 60.5 %copy-start.1 = (bf16[1,256,1024]{2,1,0:T(8,128)(2,1)S(1)}, bf16[1,256,1024]{2,1,0:T(8,128)(2,1)}, u32[]{:S(2)}) copy-start(bf16[1,256,1024]{2,1,0:T(8,128)(2,1)} %param.16) | copy-start | bytes 1572868
  24.4 110.4 %all-gather.5.cloned.1.call-start = ((), (), s32[]{:S(2)}) async-start(), calls=%async_computation.4 | async-start | bytes 5242880 | tf_op jit(solution)/shard_map/all_gather | solution.py:30
  79.9 12.7 %copy-start.7 = (f32[1,4,256]{2,1,0:T(4,128)S(1)}, f32[1,4,256]{2,1,0:T(4,128)}, u32[]{:S(2)}) copy-start(f32[1,4,256]{2,1,0:T(4,128)} %param.20) | copy-start | bytes 12292
  79.9 12.7 %copy-start.3 = (f32[1,16,256]{2,1,0:T(8,128)S(1)}, f32[1,16,256]{2,1,0:T(8,128)}, u32[]{:S(2)}) copy-start(f32[1,16,256]{2,1,0:T(8,128)} %param.17) | copy-start | bytes 49156
  79.9 12.8 %copy-start.5 = (f32[1,16]{1,0:T(1,128)S(1)}, f32[1,16]{1,0:T(1,128)}, u32[]{:S(2)}) copy-start(f32[1,16]{1,0:T(1,128)} %param.22) | copy-start | bytes 196
  79.9 13.0 %copy-start.4 = (bf16[1,256,256]{2,1,0:T(8,128)(2,1)S(1)}, bf16[1,256,256]{2,1,0:T(8,128)(2,1)}, u32[]{:S(2)}) copy-start(bf16[1,256,256]{2,1,0:T(8,128)(2,1)} %param.15) | copy-start | bytes 393220
  93.1 41.7 %copy-start = (f32[1,1,16,64,256]{4,3,2,1,0:T(8,128)S(1)}, f32[1,1,16,64,256]{4,3,2,1,0:T(8,128)}, u32[]{:S(2)}) copy-start(f32[1,1,16,64,256]{4,3,2,1,0:T(8,128)} %fusion.15) | copy-start | bytes 3145732
  93.1 41.7 %copy-start.8 = (f32[1,16]{1,0:T(1,128)S(1)}, f32[1,16]{1,0:T(1,128)}, u32[]{:S(2)}) copy-start(f32[1,16]{1,0:T(1,128)} %param.23) | copy-start | bytes 196
  140.4 3.2 copy-start.6
  143.6 24.1 %copy-start.2 = (bf16[1,1024,512]{2,1,0:T(8,128)(2,1)S(1)}, bf16[1,1024,512]{2,1,0:T(8,128)(2,1)}, u32[]{:S(2)}) copy-start(bf16[1,1024,512]{2,1,0:T(8,128)(2,1)} %param.25) | copy-start | bytes 3145732
  171.7 191.8 %all-to-all-start.2 = ((bf16[8,1024,512]{2,1,0:T(8,128)(2,1)}), bf16[8,1024,512]{2,1,0:T(8,128)(2,1)}, u32[]{:S(2)}, u32[]{:S(2)}) async-start(bf16[8,1024,512]{2,1,0:T(8,128)(2,1)} %stack.3), calls=%async_computation.2 | async-start | bytes 16777216 | tf_op jit(solution)/shard_map/all_to_all | solution.py:152
  485.5 4.8 collective-permute-start.1
Sparse Core Ops, SparseCore 0:
  24.5 55.3 all-gather.6
  83.7 51.0 all-gather.4
